TPU v7x, 1024 devices: a whole 4x4x32 slice. The times are simulated.
1024 devices in a mesh: fsdp: 64 (over y_lo, z), grp: 16 (over y_hi, x, core).
Axes of the slice: x: 4, y: 4 (y_hi: 2, y_lo: 2; y = y_hi * 2 + y_lo), z: 32, core: 2. Of those that a mesh axis runs over, the one named last changes fastest.
Arguments:
- grads: bfloat16 [16, 64, 128, 8192], P('grp', 'fsdp'), may hold values from -16 to 16
- master: float32 [128, 8192], P('fsdp', 'grp'), may hold values from -0.0625 to 0.0625
- moment_one: float32 [128, 8192], P('fsdp', 'grp'), may hold values from -0.2 to 0.2
- moment_two: float32 [128, 8192], P('fsdp', 'grp'), may hold values from 0.0001 to 0.004
Outputs:
- new_master: float32 [128, 8192], P('fsdp', 'grp')
- new_first: float32 [128, 8192], P('fsdp', 'grp')
- new_second: float32 [128, 8192], P('fsdp', 'grp')
- weights: bfloat16 [128, 8192], P('fsdp')
- copy_master: float32 [128, 8192], P('fsdp', 'grp')
- copy_first: float32 [128, 8192], P('fsdp', 'grp')
- copy_second: float32 [128, 8192], P('fsdp', 'grp')
All inputs are finite; a program needn't handle non-finite values.
Results may differ from a plain program's by a relative error of at most 0.009.
Values may be sent and summed in bfloat16 or wider, within the bound.
A program may use at most 32 MiB of HBM per device.

v0:
```python
import jax
import jax.numpy as jnp
from jax import lax
from jax.sharding import Mesh
from jax.sharding import PartitionSpec as P

GRP = ("grp_0", "grp_1", "grp_2")


beta_one = 0.9
beta_two = 0.95
learn_rate = 0.01
decay_rate = 0.1
epsilon = 1e-08
step_count = 100


def in_blocks(shard, dim, length):
    before, after = (shard.shape[:dim], shard.shape[dim + 1 :])
    return jnp.moveaxis(shard.reshape(*before, length, -1, *after), dim, 0)


def in_order(pieces, dim):
    lengths = list(pieces.shape[1:])
    lengths[dim] *= pieces.shape[0]
    return jnp.moveaxis(pieces, 0, dim).reshape(lengths)


def exchange_in_order(pieces, axes, sequence):
    lengths = [lax.axis_size(a) for a in axes]
    pieces = pieces.reshape(*lengths, *pieces.shape[1:])
    for k in sequence:
        pieces = lax.all_to_all(pieces, axes[k], split_axis=k, concat_axis=k, tiled=True)
    return pieces.reshape(-1, *pieces.shape[len(axes) :])


def core_and_chips(shard, groups, sequence, split_dim, concat_dim):
    length = lax.axis_size(groups[0]) * lax.axis_size(groups[1])
    pieces = in_blocks(shard, split_dim, length)
    return in_order(exchange_in_order(pieces, groups, sequence), concat_dim)


def sum_at_owner(shard, axis, dim):
    length = lax.axis_size(axis)
    pieces = lax.all_to_all(in_blocks(shard, dim, length), axis, 0, 0, tiled=True)
    return jnp.sum(pieces, axis=0)


def passed_along(shard, axis, by):
    length = lax.axis_size(axis)
    return lax.ppermute(shard, axis, [(i, (i + by) % length) for i in range(length)])


def from_everyone(shard, axis):
    copies = jnp.broadcast_to(shard, (lax.axis_size(axis), *shard.shape))
    return lax.all_to_all(copies, axis, split_axis=0, concat_axis=0, tiled=True)


def gather_directly(shard, axis, dim):
    return in_order(from_everyone(shard, axis), dim)


def shards(grads, master, moment_one, moment_two):
    received = core_and_chips(grads[0], (("grp_0", "grp_1"), "grp_2"), (1, 0), 2, 0)
    column_share = jnp.sum(received.astype(jnp.float32), axis=0)
    owned_grad = sum_at_owner(column_share, "fsdp", 0)
    gradient = owned_grad / (lax.axis_size("fsdp") * lax.axis_size(GRP))
    new_first = beta_one * moment_one + (1.0 - beta_one) * gradient
    new_second = beta_two * moment_two + (1.0 - beta_two) * gradient * gradient
    first_hat = new_first / (1.0 - beta_one**step_count)
    second_hat = new_second / (1.0 - beta_two**step_count)
    new_master = master - learn_rate * (
        first_hat / (jnp.sqrt(second_hat) + epsilon) + decay_rate * master
    )
    snapshot = passed_along((new_master, new_first, new_second), GRP, 1)
    weights = gather_directly(new_master.astype(jnp.bfloat16), GRP, 1)
    return (new_master, new_first, new_second, weights, snapshot[0], snapshot[1], snapshot[2])


def solution(mesh):
    finer = Mesh(
        mesh.devices.reshape(mesh.shape["fsdp"], 2, 4, 2), ("fsdp", "grp_0", "grp_1", "grp_2")
    )
    placed = (P(GRP, "fsdp", None, None), P("fsdp", GRP), P("fsdp", GRP), P("fsdp", GRP))
    return jax.shard_map(
        shards,
        mesh=finer,
        in_specs=placed,
        out_specs=(
            P("fsdp", GRP),
            P("fsdp", GRP),
            P("fsdp", GRP),
            P("fsdp", None),
            P("fsdp", GRP),
            P("fsdp", GRP),
            P("fsdp", GRP),
        ),
        check_vma=False,
    )
```

profile of v0, /device:TPU:16, one launch (start us, length us, event | category | flops | bytes accessed | tf_op | source)
XLA Modules:
  0.0 144.2 jit_solution(2783648790023009045)
XLA Ops:
  0.6 4.1 %copy.22 = bf16[1,1,128,8192]{2,3,1,0:T(8,128)(2,1)} copy(bf16[1,1,128,8192]{3,2,1,0:T(8,128)(2,1)} %param.4) | data formatting | bytes 4194304 | tf_op args[0]
  4.7 3.4 %copy.24 = bf16[8,2,1,128,512]{4,0,3,2,1:T(8,128)(2,1)S(1)} copy(bf16[8,2,1,128,512]{3,4,1,0,2:T(8,128)(2,1)} %bitcast.8) | data formatting | bytes 4194304 | tf_op jit(solution)/shard_map/reshape | solution.py:31
  8.1 5.4 %all_to_all.20 = bf16[8,2,1,128,512]{4,0,3,2,1:T(8,128)(2,1)S(1)} all-to-all(bf16[8,2,1,128,512]{4,0,3,2,1:T(8,128)(2,1)S(1)} %copy.24), channel_id=1, replica_groups=mesh['fsdp'=64,'grp_0'=2,'grp_1'=4,'grp_2'=2] {'grp_2'}, dimensions={1} | all-to-all | bytes 4194304 | tf_op jit(solution)/shard_map/all_to_all | solution.py:33
  13.5 2.2 %copy.25 = bf16[8,2,1,128,512]{4,1,3,2,0:T(2,128)(2,1)S(1)} copy(bf16[8,2,1,128,512]{4,0,3,2,1:T(8,128)(2,1)S(1)} %all_to_all.20) | data formatting | bytes 4194304 | tf_op jit(solution)/shard_map/all_to_all | solution.py:33
  15.7 41.4 %all_to_all.21 = bf16[8,2,1,128,512]{4,1,3,2,0:T(2,128)(2,1)S(1)} all-to-all(bf16[8,2,1,128,512]{4,1,3,2,0:T(2,128)(2,1)S(1)} %copy.25), channel_id=1, replica_groups=mesh['fsdp'=64,'grp_0'=2,'grp_1'=4,'grp_2'=2] {'grp_0','grp_1'}, dimensions={0} | all-to-all | bytes 4194304 | tf_op jit(solution)/shard_map/all_to_all | solution.py:33
  57.1 0.0 copy-start
  57.1 0.0 copy-start.1
  57.1 0.0 copy-start.2
  57.1 2.0 %convert_reduce_fusion = f32[128,512]{1,0:T(8,128)S(1)} fusion(bf16[8,2,1,128,512]{4,1,3,2,0:T(2,128)(2,1)S(1)} %all_to_all.21), kind=kLoop, calls=%fused_computation | loop fusion | flops 2031616 | bytes 2359296 | tf_op jit(solution)/shard_map/reduce_sum | solution.py:65
  59.2 0.1 reshape.24
  59.3 61.8 %all_to_all.22 = f32[64,2,512]{2,1,0:T(2,128)S(1)} all-to-all(f32[64,2,512]{2,1,0:T(2,128)S(1)} %reshape.24), channel_id=1, replica_groups=mesh['fsdp'=64,'grp_0'=2,'grp_1'=4,'grp_2'=2] {'fsdp'}, dimensions={0} | all-to-all | bytes 524288 | tf_op jit(solution)/shard_map/all_to_all | solution.py:45
  121.1 0.1 reduce_sum.19
  121.2 0.0 copy-done
  121.2 0.0 copy-done.1
  121.3 0.0 copy-done.2
  121.3 0.0 copy-start.3
  121.3 0.0 copy-start.4
  121.3 0.0 copy-start.5
  121.3 0.6 broadcast_in_dim.3
  122.0 5.9 %all-to-all-start.3 = ((bf16[16,2,512]{2,1,0:T(2,128)(2,1)}), bf16[16,2,512]{2,1,0:T(2,128)(2,1)S(1)}, u32[]{:S(2)}, u32[]{:S(2)}) async-start(bf16[16,2,512]{2,1,0:T(2,128)(2,1)} %broadcast_in_dim.3), calls=%async_computation.3 | async-start | bytes 65536 | tf_op jit(solution)/shard_map/all_to_all | solution.py:56
  127.9 2.0 %collective-permute-start = (f32[2,512]{1,0:T(2,128)S(1)}, f32[2,512]{1,0:T(2,128)S(1)}, u32[]{:S(2)}, u32[]{:S(2)}) collective-permute-start(f32[2,512]{1,0:T(2,128)S(1)} %get-tuple-element.18), channel_id=1, source_target_pairs={{0,1},{1,2},{2,3},{3,4},{4,5},{5,6},{6,7},{7,8},{8,9},{9,10},{10,1... | collective-permute-start | bytes 12296 | tf_op jit(solution)/shard_map/ppermute | solution.py:51
  129.9 3.4 %collective-permute-start.1 = (f32[2,512]{1,0:T(2,128)S(1)}, f32[2,512]{1,0:T(2,128)S(1)}, u32[]{:S(2)}, u32[]{:S(2)}) collective-permute-start(f32[2,512]{1,0:T(2,128)S(1)} %get-tuple-element.19), channel_id=1, source_target_pairs={{0,1},{1,2},{2,3},{3,4},{4,5},{5,6},{6,7},{7,8},{8,9},{9,10},{10,1... | collective-permute-start | bytes 12296 | tf_op jit(solution)/shard_map/ppermute | solution.py:51
  133.3 2.0 %collective-permute-start.2 = (f32[2,512]{1,0:T(2,128)S(1)}, f32[2,512]{1,0:T(2,128)S(1)}, u32[]{:S(2)}, u32[]{:S(2)}) collective-permute-start(f32[2,512]{1,0:T(2,128)S(1)} %get-tuple-element.20), channel_id=1, source_target_pairs={{0,1},{1,2},{2,3},{3,4},{4,5},{5,6},{6,7},{7,8},{8,9},{9,10},{10,1... | collective-permute-start | bytes 12296 | tf_op jit(solution)/shard_map/ppermute | solution.py:51
  135.3 1.1 collective-permute-done
  136.4 2.0 %collective-permute-done.1 = f32[2,512]{1,0:T(2,128)S(1)} collective-permute-done((f32[2,512]{1,0:T(2,128)S(1)}, f32[2,512]{1,0:T(2,128)S(1)}, u32[]{:S(2)}, u32[]{:S(2)}) %collective-permute-start.1) | collective-permute-done | bytes 4128 | tf_op jit(solution)/shard_map/ppermute | solution.py:51
  138.4 3.4 %collective-permute-done.2 = f32[2,512]{1,0:T(2,128)S(1)} collective-permute-done((f32[2,512]{1,0:T(2,128)S(1)}, f32[2,512]{1,0:T(2,128)S(1)}, u32[]{:S(2)}, u32[]{:S(2)}) %collective-permute-start.2) | collective-permute-done | bytes 4128 | tf_op jit(solution)/shard_map/ppermute | solution.py:51
  141.8 0.0 all-to-all-done.3
  141.8 0.6 copy.34
  142.4 0.6 copy.35
  143.0 0.6 copy.36
  143.6 0.6 copy.37
  144.2 0.0 copy-done.3
  144.2 0.0 copy-done.4
  144.2 0.0 copy-done.5
  (1 shorter events, 0.0 us)
Async XLA Ops:
  57.1 64.1 %copy-start = (f32[2,512]{1,0:T(2,128)S(1)}, f32[2,512]{1,0:T(2,128)}, u32[]{:S(2)}) copy-start(f32[2,512]{1,0:T(2,128)} %param.5) | copy-start | bytes 12292
  57.1 64.1 %copy-start.1 = (f32[2,512]{1,0:T(2,128)S(1)}, f32[2,512]{1,0:T(2,128)}, u32[]{:S(2)}) copy-start(f32[2,512]{1,0:T(2,128)} %param.6) | copy-start | bytes 12292
  57.1 64.1 %copy-start.2 = (f32[2,512]{1,0:T(2,128)S(1)}, f32[2,512]{1,0:T(2,128)}, u32[]{:S(2)}) copy-start(f32[2,512]{1,0:T(2,128)} %param.7) | copy-start | bytes 12292
  121.3 22.9 %copy-start.3 = (f32[2,512]{1,0:T(2,128)}, f32[2,512]{1,0:T(2,128)S(1)}, u32[]{:S(2)}) copy-start(f32[2,512]{1,0:T(2,128)S(1)} %get-tuple-element.18) | copy-start | bytes 12292
  121.3 22.9 %copy-start.4 = (f32[2,512]{1,0:T(2,128)}, f32[2,512]{1,0:T(2,128)S(1)}, u32[]{:S(2)}) copy-start(f32[2,512]{1,0:T(2,128)S(1)} %get-tuple-element.19) | copy-start | bytes 12292
  121.3 22.9 %copy-start.5 = (f32[2,512]{1,0:T(2,128)}, f32[2,512]{1,0:T(2,128)S(1)}, u32[]{:S(2)}) copy-start(f32[2,512]{1,0:T(2,128)S(1)} %get-tuple-element.20) | copy-start | bytes 12292
  122.0 19.8 %all-to-all-start.3 = ((bf16[16,2,512]{2,1,0:T(2,128)(2,1)}), bf16[16,2,512]{2,1,0:T(2,128)(2,1)S(1)}, u32[]{:S(2)}, u32[]{:S(2)}) async-start(bf16[16,2,512]{2,1,0:T(2,128)(2,1)} %broadcast_in_dim.3), calls=%async_computation.3 | async-start | bytes 65536 | tf_op jit(solution)/shard_map/all_to_all | solution.py:56
  127.9 8.5 %collective-permute-start = (f32[2,512]{1,0:T(2,128)S(1)}, f32[2,512]{1,0:T(2,128)S(1)}, u32[]{:S(2)}, u32[]{:S(2)}) collective-permute-start(f32[2,512]{1,0:T(2,128)S(1)} %get-tuple-element.18), channel_id=1, source_target_pairs={{0,1},{1,2},{2,3},{3,4},{4,5},{5,6},{6,7},{7,8},{8,9},{9,10},{10,1... | collective-permute-start | bytes 12296 | tf_op jit(solution)/shard_map/ppermute | solution.py:51
  129.9 8.5 %collective-permute-start.1 = (f32[2,512]{1,0:T(2,128)S(1)}, f32[2,512]{1,0:T(2,128)S(1)}, u32[]{:S(2)}, u32[]{:S(2)}) collective-permute-start(f32[2,512]{1,0:T(2,128)S(1)} %get-tuple-element.19), channel_id=1, source_target_pairs={{0,1},{1,2},{2,3},{3,4},{4,5},{5,6},{6,7},{7,8},{8,9},{9,10},{10,1... | collective-permute-start | bytes 12296 | tf_op jit(solution)/shard_map/ppermute | solution.py:51
  133.3 8.5 %collective-permute-start.2 = (f32[2,512]{1,0:T(2,128)S(1)}, f32[2,512]{1,0:T(2,128)S(1)}, u32[]{:S(2)}, u32[]{:S(2)}) collective-permute-start(f32[2,512]{1,0:T(2,128)S(1)} %get-tuple-element.20), channel_id=1, source_target_pairs={{0,1},{1,2},{2,3},{3,4},{4,5},{5,6},{6,7},{7,8},{8,9},{9,10},{10,1... | collective-permute-start | bytes 12296 | tf_op jit(solution)/shard_map/ppermute | solution.py:51
where the time goes:
time: 145 us; the launch traced here: 144 us
  blocking collectives  109 us (75%)
  starting transfers between devices  13.3 us (9%)
  local copies, waits for them, and re-layouts  12.8 us (9%)
  waiting for transfers between devices  6.51 us (4%)
  other arithmetic  2.18 us (2%)
    all_to_all x1, blocking collectives, sum_at_owner(): lax.all_to_all(in_blocks(shard, dim, length), axis, 0, 0, tiled=True)  61.8 us
    all_to_all x2, blocking collectives, exchange_in_order(): lax.all_to_all(pieces, axes[k], split_axis=k, concat_axis=k, tiled=True)  46.9 us
    ppermute x3, starting transfers between devices, passed_along(): lax.ppermute(shard, axis, [(i, (i + by) % length) for i in range(length)])  7.41 us
    unnamed x17, local copies, waits for them, and re-layouts  6.52 us
    ppermute x3, waiting for transfers between devices, passed_along(): lax.ppermute(shard, axis, [(i, (i + by) % length) for i in range(length)])  6.51 us
    all_to_all x1, starting transfers between devices, from_everyone(): return lax.all_to_all(copies, axis, split_axis=0, concat_axis=0, tiled=True)  5.88 us
    reshape x1, local copies, waits for them, and re-layouts, exchange_in_order(): pieces = pieces.reshape(*lengths, *pieces.shape[1:])  3.36 us
  transfers between devices with their start and end apart: 4, of which 3 were waited for; matrix products, arithmetic and copies ran while one was open for 0% of the time, Pallas kernels for 0%

commit v1 on v0

v1 whole, which is shorter than its diff:
```python
import functools

import jax
import jax.numpy as jnp
from jax import lax
from jax.experimental import pallas as pl
from jax.experimental.pallas import tpu as pltpu
from jax.sharding import PartitionSpec as P

MESH = pl.DeviceIdType.MESH

beta_one = 0.9
beta_two = 0.95
learn_rate = 0.01
decay_rate = 0.1
epsilon = 1e-08
step_count = 100

N_X, N_Y, N_Y_LO, N_CORE = 4, 4, 2, 2
LANES = 128


def add(*terms):
    total = terms[0].astype(jnp.float32)
    for term in terms[1:]:
        total = total + term.astype(jnp.float32)
    return total


def kernel(
    n_z, n_grp, n_fsdp,
    grads, master, first, second,
    new_master, new_first, new_second, weights, copy_master, copy_first, copy_second,
    own, other, one_up, one_down, two_up, two_down,
    part, late_one_up, late_one_down, late_two_up, late_two_down,
    flat, leaving, arriving, total,
    own_sem, other_sem, other_sent, ring_sem, ring_sent, late_sem, late_sent,
    far_sem, far_sent, weights_sem, weights_sent, copy_sem, copy_sent, known_sem,
):
    f, g = lax.axis_index("fsdp"), lax.axis_index("grp")
    z, y_lo = lax.rem(f, n_z), f // n_z
    core, x, y_hi = lax.rem(g, N_CORE), lax.rem(g // N_CORE, N_X), g // (N_CORE * N_X)
    y = y_hi * N_Y_LO + y_lo
    half_rows, width = own.shape[-2:]

    def device(dx=0, dy=0, dz=0, flip=False):
        to_x, to_y = lax.rem(x + dx + N_X, N_X), lax.rem(y + dy + N_Y, N_Y)
        to_z = lax.rem(z + dz + n_z, n_z)
        to_core = 1 - core if flip else core
        return (
            lax.rem(to_y, N_Y_LO) * n_z + to_z,
            ((to_y // N_Y_LO) * N_X + to_x) * N_CORE + to_core,
        )

    def send(source, target, sent, received, to):
        copy = pltpu.make_async_remote_copy(
            src_ref=source, dst_ref=target, send_sem=sent, recv_sem=received,
            device_id=to, device_id_type=MESH,
        )
        copy.start()

    def await_bytes(ref, sem):
        pltpu.make_async_copy(ref, ref, sem).wait()

    def tell(sem, to):
        pl.semaphore_signal(sem, inc=1, device_id=to, device_id_type=MESH)

    def block(a, k, j, of_core):
        dx, dy = (k, j) if a == 0 else (j, k)
        to_x, to_y = lax.rem(x + dx, N_X), lax.rem(y + dy, N_Y)
        owner = ((to_y // N_Y_LO) * N_X + to_x) * N_CORE + of_core
        column = pl.multiple_of(owner * width, width)
        return grads.at[
            lax.rem(to_y, N_Y_LO), pl.ds(a * half_rows, half_rows), pl.ds(column, width)
        ]

    order = (2, 1, 3, 0)
    near = [
        device(flip=True), device(dx=1), device(dx=-1), device(dy=1), device(dy=-1),
        device(dz=1), device(dz=-1),
    ]
    barrier = pltpu.get_barrier_semaphore()
    for to in near:
        tell(barrier, to)
    for k in order:
        for a in range(2):
            for j in range(4):
                pltpu.make_async_copy(
                    block(a, k, j, core), own.at[a, k, j], own_sem.at[a, k]
                ).start()
    pl.semaphore_wait(barrier, len(near))

    for k in order:
        for a in range(2):
            for j in range(4):
                send(
                    block(a, k, j, 1 - core), other.at[a, k, j],
                    other_sent, other_sem.at[a, k], near[0],
                )

    strides = [1 << i for i in range(known_sem.shape[0])]

    def tell_far(i):
        for step in (strides[i], -strides[i]):
            tell(known_sem.at[i], device(dz=step))

    def await_far(i):
        pl.semaphore_wait(known_sem.at[i], 2)

    up = (device(dx=1), device(dy=1))
    down = (device(dx=-1), device(dy=-1))

    def both_cores(a, k):
        await_bytes(own.at[a, k], own_sem.at[a, k])
        await_bytes(other.at[a, k], other_sem.at[a, k])
        own[a, k] = add(own[a, k], other[a, k]).astype(own.dtype)

    tell_far(0)
    await_far(0)
    tell_far(1)
    for a in range(2):
        both_cores(a, 2)
        send(own.at[a, 2, 0:2], one_up.at[a], ring_sent.at[a, 0], ring_sem.at[a, 0], up[a])
        send(own.at[a, 2, 2:4], one_down.at[a], ring_sent.at[a, 1], ring_sem.at[a, 1], down[a])
    await_far(1)
    tell_far(2)
    for a in range(2):
        both_cores(a, 1)
        send(own.at[a, 1, 2:4], two_up.at[a, 2:4], ring_sent.at[a, 2], ring_sem.at[a, 2], up[a])
        both_cores(a, 3)
        send(own.at[a, 3, 0:2], two_down.at[a, 0:2], ring_sent.at[a, 3], ring_sem.at[a, 3], down[a])
    for a in range(2):
        await_bytes(one_up.at[a], ring_sem.at[a, 0])
        own[a, 1, 0:2] = add(own[a, 1, 0:2], one_up[a]).astype(own.dtype)
        send(own.at[a, 1, 0:2], two_up.at[a, 0:2], ring_sent.at[a, 4], ring_sem.at[a, 4], up[a])
        await_bytes(one_down.at[a], ring_sem.at[a, 1])
        own[a, 3, 2:4] = add(own[a, 3, 2:4], one_down[a]).astype(own.dtype)
        send(own.at[a, 3, 2:4], two_down.at[a, 2:4], ring_sent.at[a, 5], ring_sem.at[a, 5], down[a])
    await_far(2)
    tell_far(3)
    for a in range(2):
        both_cores(a, 0)
    for a in range(2):
        await_bytes(two_up.at[a, 2:4], ring_sem.at[a, 2])
        await_bytes(two_down.at[a, 0:2], ring_sem.at[a, 3])
        await_bytes(two_up.at[a, 0:2], ring_sem.at[a, 4])
        await_bytes(two_down.at[a, 2:4], ring_sem.at[a, 5])
        part[a, 2] = add(own[a, 0, 2], two_up[a, 2], two_down[a, 2]).astype(part.dtype)
        mid = half_rows // 2
        send(part.at[a, 2, 0:mid], late_one_up.at[a], late_sent.at[a, 0], late_sem.at[a, 0], up[1 - a])
        send(part.at[a, 2, mid:], late_one_down.at[a], late_sent.at[a, 1], late_sem.at[a, 1], down[1 - a])
        for j in (1, 3, 0):
            part[a, j] = add(own[a, 0, j], two_up[a, j], two_down[a, j]).astype(part.dtype)
        send(part.at[a, 1, mid:], late_two_up.at[a, mid:], late_sent.at[a, 2], late_sem.at[a, 2], up[1 - a])
        send(part.at[a, 3, 0:mid], late_two_down.at[a, 0:mid], late_sent.at[a, 3], late_sem.at[a, 3], down[1 - a])
    for a in range(2):
        await_bytes(late_one_up.at[a], late_sem.at[a, 0])
        part[a, 1, 0:mid] = add(part[a, 1, 0:mid], late_one_up[a]).astype(part.dtype)
        send(part.at[a, 1, 0:mid], late_two_up.at[a, 0:mid], late_sent.at[a, 4], late_sem.at[a, 4], up[1 - a])
        await_bytes(late_one_down.at[a], late_sem.at[a, 1])
        part[a, 3, mid:] = add(part[a, 3, mid:], late_one_down[a]).astype(part.dtype)
        send(part.at[a, 3, mid:], late_two_down.at[a, mid:], late_sent.at[a, 5], late_sem.at[a, 5], down[1 - a])
    pieces = n_z // 2
    for a in range(2):
        await_bytes(late_two_up.at[a, mid:], late_sem.at[a, 2])
        await_bytes(late_two_down.at[a, 0:mid], late_sem.at[a, 3])
        await_bytes(late_two_up.at[a, 0:mid], late_sem.at[a, 4])
        await_bytes(late_two_down.at[a, mid:], late_sem.at[a, 5])
        plane = add(part[a, 0], late_two_up[a], late_two_down[a])
        for t in range(width // LANES):
            flat[a, pl.ds(t, half_rows, stride=width // LANES), :] = plane[:, t * LANES:(t + 1) * LANES]
        leaving[a * pieces:(a + 1) * pieces] = (
            flat[a].reshape(pieces, *leaving.shape[1:]).astype(leaving.dtype)
        )
    await_far(3)
    far = [n_z // 2]
    for d in range(n_z // 2 - 1, 0, -1):
        far += [d, n_z - d]
    for d in far:
        to_z = lax.rem(z + d, n_z)
        send(leaving.at[to_z], arriving.at[d - 1], far_sent, far_sem, device(dz=d))

    await_bytes(arriving, far_sem)
    total[...] = add(leaving[z], *[arriving[d] for d in range(n_z - 1)])

    scale = 1.0 / (n_grp * n_fsdp)
    for t in range(width // LANES):
        at = slice(t * LANES, (t + 1) * LANES)
        gradient = total[pl.ds(t, 2, stride=width // LANES), :] * scale
        one = beta_one * first[:, at] + (1.0 - beta_one) * gradient
        two = beta_two * second[:, at] + (1.0 - beta_two) * gradient * gradient
        one_hat = one / (1.0 - beta_one**step_count)
        two_hat = two / (1.0 - beta_two**step_count)
        old = master[:, at]
        new = old - learn_rate * (one_hat / (jnp.sqrt(two_hat) + epsilon) + decay_rate * old)
        new_master[:, at] = new
        new_first[:, at] = one
        new_second[:, at] = two
    mine = pl.ds(pl.multiple_of(g * width, width), width)
    weights[:, mine] = new_master[...].astype(weights.dtype)
    after = (f, lax.rem(g + 1, n_grp))
    for i in range(n_grp - 1, 0, -1):
        to = lax.rem(g + i, n_grp)
        send(weights.at[:, mine], weights.at[:, mine], weights_sent.at[i - 1], weights_sem.at[i - 1], (f, to))
    for i, (new, copied) in enumerate(
        ((new_master, copy_master), (new_first, copy_first), (new_second, copy_second))
    ):
        send(new, copied, copy_sent.at[i], copy_sem.at[i], after)

    await_bytes(other, other_sent)
    for a in range(2):
        for i, ref in enumerate((one_up.at[a], one_down.at[a], one_up.at[a], one_up.at[a], one_up.at[a], one_up.at[a])):
            await_bytes(ref, ring_sent.at[a, i])
        for i in range(6):
            await_bytes(late_one_up.at[a], late_sent.at[a, i])
    await_bytes(arriving, far_sent)
    for i in range(1, n_grp):
        source = lax.rem(g - i + n_grp, n_grp)
        theirs = pl.ds(pl.multiple_of(source * width, width), width)
        await_bytes(weights.at[:, theirs], weights_sem.at[i - 1])
        await_bytes(weights.at[:, mine], weights_sent.at[i - 1])
    for i, (new, copied) in enumerate(
        ((new_master, copy_master), (new_first, copy_first), (new_second, copy_second))
    ):
        await_bytes(copied, copy_sem.at[i])
        await_bytes(new, copy_sent.at[i])


def shards(n_fsdp, n_grp, grads, master, moment_one, moment_two):
    rows, columns = grads.shape[2:]
    n_z = n_fsdp // N_Y_LO
    width = columns // n_grp
    half_rows = rows // (2 * N_Y_LO)
    mid = half_rows // 2
    piece = (rows // n_fsdp) * width // LANES
    vmem = pl.BlockSpec(memory_space=pltpu.VMEM)
    small = jax.ShapeDtypeStruct(master.shape, jnp.float32)
    wide = jax.ShapeDtypeStruct((master.shape[0], columns), jnp.bfloat16)
    bf16, f32, dma = jnp.bfloat16, jnp.float32, pltpu.SemaphoreType.DMA
    return pl.pallas_call(
        functools.partial(kernel, n_z, n_grp, n_fsdp),
        out_shape=(small, small, small, wide, small, small, small),
        in_specs=[pl.BlockSpec(memory_space=pl.ANY), vmem, vmem, vmem],
        out_specs=[vmem] * 7,
        scratch_shapes=[
            pltpu.VMEM((2, 4, 4, half_rows, width), bf16),
            pltpu.VMEM((2, 4, 4, half_rows, width), bf16),
            pltpu.VMEM((2, 2, half_rows, width), bf16),
            pltpu.VMEM((2, 2, half_rows, width), bf16),
            pltpu.VMEM((2, 4, half_rows, width), bf16),
            pltpu.VMEM((2, 4, half_rows, width), bf16),
            pltpu.VMEM((2, 4, half_rows, width), bf16),
            pltpu.VMEM((2, mid, width), bf16),
            pltpu.VMEM((2, mid, width), bf16),
            pltpu.VMEM((2, half_rows, width), bf16),
            pltpu.VMEM((2, half_rows, width), bf16),
            pltpu.VMEM((2, half_rows * width // LANES, LANES), f32),
            pltpu.VMEM((n_z, piece, LANES), bf16),
            pltpu.VMEM((n_z - 1, piece, LANES), bf16),
            pltpu.VMEM((piece, LANES), f32),
            dma((2, 4)), dma((2, 4)), dma,
            dma((2, 6)), dma((2, 6)), dma((2, 6)), dma((2, 6)),
            dma, dma,
            dma((n_grp - 1,)), dma((n_grp - 1,)), dma((3,)), dma((3,)),
            pltpu.SemaphoreType.REGULAR((n_z.bit_length() - 2,)),
        ],
        compiler_params=pltpu.CompilerParams(
            collective_id=0, has_side_effects=True, vmem_limit_bytes=16 << 20
        ),
        name="step",
    )(grads.reshape(N_Y_LO, rows // N_Y_LO, columns), master, moment_one, moment_two)


def solution(mesh):
    return jax.shard_map(
        functools.partial(shards, mesh.shape["fsdp"], mesh.shape["grp"]),
        mesh=mesh,
        in_specs=(P("grp", "fsdp", None, None), P("fsdp", "grp"), P("fsdp", "grp"), P("fsdp", "grp")),
        out_specs=(
            P("fsdp", "grp"), P("fsdp", "grp"), P("fsdp", "grp"), P("fsdp", None),
            P("fsdp", "grp"), P("fsdp", "grp"), P("fsdp", "grp"),
        ),
        check_vma=False,
    )
```

time: 145 us -> 66.1 us (0.46)
  the two profiles are of different devices: /device:TPU:16 before, /device:TPU:1 now
where the time goes in v1:
time: 66.1 us; the launch traced here: 65.8 us
  Pallas kernels  57.3 us (87%)
  local copies, waits for them, and re-layouts  7.81 us (12%)
    pallas_call x1, Pallas kernels, shards(): pl.pallas_call(functools.partial(kernel, n_z, n_grp, n_fsdp), out_shape=(...  57.3 us
    unnamed x15, local copies, waits for them, and re-layouts  7.81 us

profile of v1, /device:TPU:1, one launch (start us, length us, event | category | flops | bytes accessed | tf_op | source)
XLA Modules:
  0.0 65.8 jit_solution(1491317161725057042)
XLA Ops:
  0.6 0.0 copy-start
  0.6 1.6 %copy-done = bf16[1,1,128,8192]{3,2,1,0:T(8,128)(2,1)S(1)} copy-done((bf16[1,1,128,8192]{3,2,1,0:T(8,128)(2,1)S(1)}, bf16[1,1,128,8192]{3,2,1,0:T(8,128)(2,1)}, u32[]{:S(2)}) %copy-start) | copy-done | bytes 2097176
  2.2 0.0 copy-start.1
  2.2 0.7 %copy-done.1 = f32[2,512]{1,0:T(2,128)S(1)} copy-done((f32[2,512]{1,0:T(2,128)S(1)}, f32[2,512]{1,0:T(2,128)}, u32[]{:S(2)}) %copy-start.1) | copy-done | bytes 4120
  2.9 0.0 copy-start.2
  2.9 0.7 %copy-done.2 = f32[2,512]{1,0:T(2,128)S(1)} copy-done((f32[2,512]{1,0:T(2,128)S(1)}, f32[2,512]{1,0:T(2,128)}, u32[]{:S(2)}) %copy-start.2) | copy-done | bytes 4120
  3.6 0.0 copy-start.3
  3.6 0.7 %copy-done.3 = f32[2,512]{1,0:T(2,128)S(1)} copy-done((f32[2,512]{1,0:T(2,128)S(1)}, f32[2,512]{1,0:T(2,128)}, u32[]{:S(2)}) %copy-start.3) | copy-done | bytes 4120
  4.3 57.3 %step.1 = (f32[2,512]{1,0:T(2,128)S(1)}, f32[2,512]{1,0:T(2,128)S(1)}, f32[2,512]{1,0:T(2,128)S(1)}, bf16[2,8192]{1,0:T(2,128)(2,1)S(1)}, f32[2,512]{1,0:T(2,128...) custom-call(bf16[2,64,8192]{2,1,0:T(8,128)(2,1)S(1)} %bitcast.1, f32[2,512]{1,0:T(2,128)S(1)} %copy-done.1, ...), custom_call_target="tpu_custom_call" | custom-call | tf_op jit(solution)/shard_map/step/pallas_call | solution.py:240
  61.6 0.6 copy.18
  62.2 0.6 copy.19
  62.8 0.6 copy.20
  63.4 0.6 copy.21
  64.0 0.6 copy.22
  64.6 0.6 copy.23
  65.2 0.6 copy.24
Async XLA Ops:
  0.6 1.6 %copy-start = (bf16[1,1,128,8192]{3,2,1,0:T(8,128)(2,1)S(1)}, bf16[1,1,128,8192]{3,2,1,0:T(8,128)(2,1)}, u32[]{:S(2)}) copy-start(bf16[1,1,128,8192]{3,2,1,0:T(8,128)(2,1)} %param.4) | copy-start | bytes 6291460
  2.2 0.7 %copy-start.1 = (f32[2,512]{1,0:T(2,128)S(1)}, f32[2,512]{1,0:T(2,128)}, u32[]{:S(2)}) copy-start(f32[2,512]{1,0:T(2,128)} %master.1) | copy-start | bytes 12292
  2.9 0.7 %copy-start.2 = (f32[2,512]{1,0:T(2,128)S(1)}, f32[2,512]{1,0:T(2,128)}, u32[]{:S(2)}) copy-start(f32[2,512]{1,0:T(2,128)} %first.1) | copy-start | bytes 12292
  3.6 0.7 %copy-start.3 = (f32[2,512]{1,0:T(2,128)S(1)}, f32[2,512]{1,0:T(2,128)}, u32[]{:S(2)}) copy-start(f32[2,512]{1,0:T(2,128)} %second.1) | copy-start | bytes 12292

commit v2 on v0

v2 whole, which is shorter than its diff:
```python
import functools

import jax
import jax.numpy as jnp
from jax import lax
from jax.experimental import pallas as pl
from jax.experimental.pallas import tpu as pltpu
from jax.sharding import PartitionSpec as P

MESH = pl.DeviceIdType.MESH

beta_one = 0.9
beta_two = 0.95
learn_rate = 0.01
decay_rate = 0.1
epsilon = 1e-08
step_count = 100

N_X, N_Y, N_Y_LO, N_Y_HI, N_CORE = 4, 4, 2, 2, 2
LANES = 128
CHUNK_ROWS = 8
ORDER = (
    ("X", 0), ("E", 0), ("X", 1), ("X", 2), ("X", 3), ("X", 4), ("X", 5), ("X", 6), ("X", 7), ("E", 1), ("W", 0), ("E", 2),
    ("Q", 0), ("W", 1), ("E", 3), ("Q", 1), ("E", 4), ("Z", 0), ("W", 2), ("E", 5), ("Q", 2), ("E", 6), ("Z", 1), ("Q", 3), ("E", 7), ("Q", 4),
    ("W", 3), ("Z", 2), ("Q", 5), ("Z", 3), ("Q", 6), ("Z", 4), ("Q", 7), ("Z", 5), ("Z", 6), ("Z", 7),
)
GREETERS = 8


def add(*terms):
    total = terms[0].astype(jnp.float32)
    for term in terms[1:]:
        total = total + term.astype(jnp.float32)
    return total


def await_bytes(ref, sem):
    pltpu.make_async_copy(ref, ref, sem).wait()


def kernel(
    n_z, n_grp, n_fsdp,
    grads, master_in, first_in, second_in,
    new_master, new_first, new_second, weights, copy_master, copy_first, copy_second,
    raw, other, own, early, part, late, flat, leaving, arriving, relayed, passing, passed, total, state,
    raw_sem, state_sem, other_sem, other_sent, early_sem, early_sent, late_sem, late_sent,
    far_sem, far_sent, relay_sem, pass_sem, pass_sent, weights_sem, weights_sent, copy_sem, copy_sent, known_sem,
):
    f, g = lax.axis_index("fsdp"), lax.axis_index("grp")
    z, y_lo = lax.rem(f, n_z), f // n_z
    core, x, y_hi = lax.rem(g, N_CORE), lax.rem(g // N_CORE, N_X), g // (N_CORE * N_X)
    y = y_hi * N_Y_LO + y_lo
    width = own.shape[-1]
    half = width // 2
    n_chunks = raw.shape[0]
    per_chunk = n_z // n_chunks

    def device(dx=0, dy=0, dz=0, flip=False):
        to_x, to_y = lax.rem(x + dx + N_X, N_X), lax.rem(y + dy + N_Y, N_Y)
        to_z = lax.rem(z + dz + n_z, n_z)
        to_core = 1 - core if flip else core
        return (
            lax.rem(to_y, N_Y_LO) * n_z + to_z,
            ((to_y // N_Y_LO) * N_X + to_x) * N_CORE + to_core,
        )

    def send(source, target, sent, received, to):
        pltpu.make_async_remote_copy(
            src_ref=source, dst_ref=target, send_sem=sent, recv_sem=received,
            device_id=to, device_id_type=MESH,
        ).start()

    def tell(sem, to):
        pl.semaphore_signal(sem, inc=1, device_id=to, device_id_type=MESH)

    def rows_of(to_y_hi):
        return slice(to_y_hi * N_Y_LO, (to_y_hi + 1) * N_Y_LO)

    def columns(to_y_hi, to_x, of_core):
        owner = (to_y_hi * N_X + to_x) * N_CORE + of_core
        return pl.ds(pl.multiple_of(owner * width, width), width)

    near = [
        device(flip=True), device(dx=1), device(dx=-1), device(dy=1), device(dy=-1),
        device(dz=1), device(dz=-1), device(dx=2), device(dy=2),
    ]
    def fetch(c):
        pltpu.make_async_copy(grads.at[:, c], raw.at[c], raw_sem.at[c]).start()

    fetch(0)
    barrier = pltpu.get_barrier_semaphore()
    for to in near:
        tell(barrier, to)

    first = jnp.logical_and(g == 0, y_lo == 0)
    later = jnp.logical_and(first, z != 0)
    root, helper = jnp.logical_and(first, z == 0), jnp.logical_and(first, z == 1)

    @pl.when(jnp.logical_and(z < GREETERS, jnp.logical_not(root)))
    def _():
        for d in range(1, n_z):
            tell(barrier, device(dz=d))

    for c in range(1, n_chunks):
        fetch(c)
    for i, source in enumerate((master_in, first_in, second_in)):
        pltpu.make_async_copy(source, state.at[i], state_sem).start()
    await_bytes(raw.at[0], raw_sem.at[0])
    greeted = jnp.where(z < GREETERS, GREETERS - 1, GREETERS) - jnp.where(later, 1, 0)
    pl.semaphore_wait(barrier, greeted + len(near))

    def exchange(c):
        if c:
            await_bytes(raw.at[c], raw_sem.at[c])
        for to_y_hi in range(N_Y_HI):
            for to_x in range(N_X):
                send(
                    raw.at[c, :, :, columns(to_y_hi, to_x, 1 - core)], other.at[c, rows_of(to_y_hi), to_x],
                    other_sent, other_sem.at[c], near[0],
                )

    n_known = known_sem.shape[0]

    def tell_far(i):
        for step in (1 << i, -(1 << i)):
            tell(known_sem.at[i], device(dz=step))

    def await_far(i):
        pl.semaphore_wait(known_sem.at[i], 2)
        if i + 1 < n_known:
            tell_far(i + 1)

    def both_cores(c):
        await_bytes(other.at[c], other_sem.at[c])
        for to_y_hi in range(N_Y_HI):
            for to_x in range(N_X):
                own[c, rows_of(to_y_hi), to_x] = add(
                    raw[c, :, :, columns(to_y_hi, to_x, core)], other[c, rows_of(to_y_hi), to_x]
                ).astype(own.dtype)
        for k in (2, 1, 3):
            to_x, to_y = lax.rem(x + k, N_X), lax.rem(y + k, N_Y)
            send(own.at[c, :, to_x, :, 0:half], early.at[c, 0, k - 1], early_sent, early_sem.at[c], device(dx=k))
            send(own.at[c, to_y, :, :, half:], early.at[c, 1, k - 1], early_sent, early_sem.at[c], device(dy=k))

    def second_axis(c):
        await_bytes(early.at[c], early_sem.at[c])
        for i in range(N_Y):
            part[c, 0, i] = add(own[c, i, x, :, 0:half], *[early[c, 0, k, i] for k in range(3)]).astype(part.dtype)
        for i in range(N_X):
            part[c, 1, i] = add(own[c, y, i, :, half:], *[early[c, 1, k, i] for k in range(3)]).astype(part.dtype)
        for k in (2, 1, 3):
            to_x, to_y = lax.rem(x + k, N_X), lax.rem(y + k, N_Y)
            send(part.at[c, 0, to_y], late.at[c, 0, k - 1], late_sent, late_sem.at[c], device(dy=k))
            send(part.at[c, 1, to_x], late.at[c, 1, k - 1], late_sent, late_sem.at[c], device(dx=k))

    def send_far(to_z, allowed):
        @pl.when(allowed)
        def _():
            d = lax.rem(to_z - z + n_z, n_z)
            send(leaving.at[to_z], arriving.at[d - 1], far_sent, far_sem, device(dz=d))

    def along_z(c):
        await_bytes(late.at[c], late_sem.at[c])
        ours = (part[c, 0, y], part[c, 1, x])
        tiles = width // LANES
        for a in range(2):
            plane = add(ours[a], *[late[c, a, k] for k in range(3)])
            for t in range(tiles // 2):
                flat[c, pl.ds(a * (tiles // 2) + t, CHUNK_ROWS, stride=tiles), :] = (
                    plane[:, t * LANES:(t + 1) * LANES]
                )
        leaving[c * per_chunk:(c + 1) * per_chunk] = (
            flat[c].reshape(per_chunk, *leaving.shape[1:]).astype(leaving.dtype)
        )
        for to_z in range(c * per_chunk, (c + 1) * per_chunk):
            allowed = z != to_z
            if to_z == 0:
                allowed = jnp.logical_and(allowed, jnp.logical_not(first))
            send_far(to_z, allowed)
        if c == 0:
            @pl.when(jnp.logical_and(first, z >= 2))
            def _():
                send(leaving.at[0], relayed.at[z - 2], far_sent, relay_sem, device(dz=1 - z))

    tell_far(0)
    steps = {"X": exchange, "E": both_cores, "Q": second_axis, "Z": along_z, "W": await_far}
    for step, i in ORDER:
        steps[step](i)

    await_bytes(state, state_sem)

    @pl.when(helper)
    def _():
        await_bytes(relayed, relay_sem)
        passing[...] = add(leaving[0], *[relayed[i] for i in range(n_z - 2)])
        send(passing, passed, pass_sent, pass_sem, device(dz=-1))

    @pl.when(root)
    def _():
        await_bytes(passed, pass_sem)
        total[...] = add(leaving[0], passed[...])

    @pl.when(jnp.logical_not(root))
    def _():
        await_bytes(arriving, far_sem)
        total[...] = add(leaving[z], *[arriving[d] for d in range(n_z - 1)])

    scale = 1.0 / (n_grp * n_fsdp)
    for t in range(width // LANES):
        at = slice(t * LANES, (t + 1) * LANES)
        gradient = total[pl.ds(t, 2, stride=width // LANES), :] * scale
        one = beta_one * state[1, :, at] + (1.0 - beta_one) * gradient
        two = beta_two * state[2, :, at] + (1.0 - beta_two) * gradient * gradient
        one_hat = one / (1.0 - beta_one**step_count)
        two_hat = two / (1.0 - beta_two**step_count)
        old = state[0, :, at]
        new = old - learn_rate * (one_hat / (jnp.sqrt(two_hat) + epsilon) + decay_rate * old)
        new_master[:, at] = new
        new_first[:, at] = one
        new_second[:, at] = two
    mine = pl.ds(pl.multiple_of(g * width, width), width)
    weights[:, mine] = new_master[...].astype(weights.dtype)
    after = (f, lax.rem(g + 1, n_grp))
    for i in range(n_grp - 1, 0, -1):
        to = lax.rem(g + i, n_grp)
        send(weights.at[:, mine], weights.at[:, mine], weights_sent, weights_sem, (f, to))
    copies = ((new_master, copy_master), (new_first, copy_first), (new_second, copy_second))
    for new, copied in copies:
        send(new, copied, copy_sent, copy_sem, after)

    await_bytes(other, other_sent)
    await_bytes(early, early_sent)
    await_bytes(late, late_sent)


    @pl.when(helper)
    def _():
        await_bytes(arriving.at[1:], far_sent)
        await_bytes(passing, pass_sent)

    @pl.when(jnp.logical_not(helper))
    def _():
        await_bytes(arriving, far_sent)

    others = weights.at[:, 0:(n_grp - 1) * width]
    await_bytes(others, weights_sem)
    await_bytes(others, weights_sent)
    await_bytes(state, copy_sem)
    await_bytes(state, copy_sent)


def put_out(*refs):
    n = len(refs) // 2
    sem = refs[-1]
    copies = [pltpu.make_async_copy(refs[i], refs[n + i], sem.at[i]) for i in range(n)]
    for copy in copies:
        copy.start()
    for copy in copies:
        copy.wait()


def shards(n_fsdp, n_grp, grads, master, moment_one, moment_two):
    rows, columns = grads.shape[2:]
    n_z = n_fsdp // N_Y_LO
    width = columns // n_grp
    half = width // 2
    n_chunks = rows // (N_Y_LO * CHUNK_ROWS)
    piece = (rows // n_fsdp) * width // LANES
    vmem = pl.BlockSpec(memory_space=pltpu.VMEM)
    hbm = pl.BlockSpec(memory_space=pltpu.HBM)
    small = jax.ShapeDtypeStruct(master.shape, jnp.float32)
    wide = jax.ShapeDtypeStruct((master.shape[0], columns), jnp.bfloat16)
    outputs = (small, small, small, wide, small, small, small)
    bf16, f32, dma = jnp.bfloat16, jnp.float32, pltpu.SemaphoreType.DMA
    r = CHUNK_ROWS
    results = pl.pallas_call(
        functools.partial(kernel, n_z, n_grp, n_fsdp),
        out_shape=[pltpu.VMEM(o.shape, o.dtype) for o in outputs],
        in_specs=[hbm] * 4,
        out_specs=[vmem] * 7,
        scratch_shapes=[
            pltpu.VMEM((n_chunks, N_Y_LO, r, columns), bf16),
            pltpu.VMEM((n_chunks, N_Y, N_X, r, width), bf16),
            pltpu.VMEM((n_chunks, N_Y, N_X, r, width), bf16),
            pltpu.VMEM((n_chunks, 2, 3, N_X, r, half), bf16),
            pltpu.VMEM((n_chunks, 2, N_X, r, half), bf16),
            pltpu.VMEM((n_chunks, 2, 3, r, half), bf16),
            pltpu.VMEM((n_chunks, r * width // LANES, LANES), f32),
            pltpu.VMEM((n_z, piece, LANES), bf16),
            pltpu.VMEM((n_z - 1, piece, LANES), bf16),
            pltpu.VMEM((n_z - 2, piece, LANES), bf16),
            pltpu.VMEM((piece, LANES), f32), pltpu.VMEM((piece, LANES), f32), pltpu.VMEM((piece, LANES), f32),
            pltpu.VMEM((3, *master.shape), f32),
            dma((n_chunks,)), dma, dma((n_chunks,)), dma,
            dma((n_chunks,)), dma, dma((n_chunks,)), dma,
            dma, dma, dma, dma, dma,
            dma, dma, dma, dma,
            pltpu.SemaphoreType.REGULAR((n_z.bit_length() - 2,)),
        ],
        compiler_params=pltpu.CompilerParams(
            collective_id=0, has_side_effects=True, vmem_limit_bytes=16 << 20
        ),
        name="step",
    )(*[
        pltpu.with_memory_space_constraint(a, pltpu.HBM)
        for a in (grads.reshape(N_Y_LO, n_chunks, r, columns), master, moment_one, moment_two)
    ])
    return pl.pallas_call(
        put_out,
        out_shape=outputs,
        in_specs=[vmem] * 7,
        out_specs=[pl.BlockSpec(memory_space=pltpu.HBM)] * 7,
        scratch_shapes=[dma((7,))],
        compiler_params=pltpu.CompilerParams(vmem_limit_bytes=1 << 20),
        name="put_out",
    )(*results)


def solution(mesh):
    return jax.shard_map(
        functools.partial(shards, mesh.shape["fsdp"], mesh.shape["grp"]),
        mesh=mesh,
        in_specs=(P("grp", "fsdp", None, None), P("fsdp", "grp"), P("fsdp", "grp"), P("fsdp", "grp")),
        out_specs=(
            P("fsdp", "grp"), P("fsdp", "grp"), P("fsdp", "grp"), P("fsdp", None),
            P("fsdp", "grp"), P("fsdp", "grp"), P("fsdp", "grp"),
        ),
        check_vma=False,
    )
```

time: 145 us -> 48.8 us (0.34)
  the two profiles are of different devices: /device:TPU:16 before, /device:TPU:1 now
where the time goes in v2:
time: 48.8 us; the launch traced here: 48.6 us
  Pallas kernels  48 us (98%)
  between operations  0.64 us (1%)
    pallas_call x1, Pallas kernels, shards(): pl.pallas_call(functools.partial(kernel, n_z, n_grp, n_fsdp), out_shape=[...  47.3 us

profile of v2, /device:TPU:1, one launch (start us, length us, event | category | flops | bytes accessed | tf_op | source)
XLA Modules:
  0.0 48.6 jit_solution(602504723813193769)
XLA Ops:
  0.6 47.3 %step.1 = (f32[2,512]{1,0:T(2,128)S(1)}, f32[2,512]{1,0:T(2,128)S(1)}, f32[2,512]{1,0:T(2,128)S(1)}, bf16[2,8192]{1,0:T(2,128)(2,1)S(1)}, f32[2,512]{1,0:T(2,128...) custom-call(bf16[2,8,8,8192]{3,2,1,0:T(8,128)(2,1)} %bitcast.1, f32[2,512]{1,0:T(2,128)} %master_in.1, ...), custom_call_target="tpu_custom_call" | custom-call | tf_op jit(solution)/shard_map/step/pallas_call | solution.py:276
  47.9 0.7 %put_out.1 = (f32[2,512]{1,0:T(2,128)}, f32[2,512]{1,0:T(2,128)}, f32[2,512]{1,0:T(2,128)}, bf16[2,8192]{1,0:T(2,128)(2,1)}, f32[2,512]{1,0:T(2,128)}, /*index=5*/f32[2,512]{1,0:T(2,128)}, f32[2,512]{1,0:T(2,128)}) custom-call(f32[2,512]{1,0:T(2,128)S(1)} %get-tuple-element.14.refs_0_, f32[2,512]{1,0:T(2,128)S(1)} %get-tuple-element.15.refs_1_, ...), custom_call_target="tpu_custom_call" | custom-call | tf_op jit(solution)/shard_map/put_out/pallas_call | solution.py:308
